TPU v7x, 32 devices: a whole 2x2x4 slice. The times are simulated.
32 devices in a mesh: radial: 8 (over z, x), phi: 4 (over y, core).
Axes of the slice: x: 2, y: 2, z: 4, core: 2. Of those that a mesh axis runs over, the one named last changes fastest.
Arguments:
- conserved: float32 [8, 64, 64, 128], P(None, 'radial', 'phi'), may hold values from -2.5 to 7, as said below
- core_mass: float32 [1], replicated, may hold values from 0.2 to 1
Outputs:
- advanced: float32 [8, 64, 64, 128], P(None, 'radial', 'phi')
- enclosed_mass: float32 [64], P('radial')
Inputs may be any that keep to these rules, and one draw needn't show every extreme that they name: conserved[0] (density) lies between 0.4 and 2.5; conserved[4] exceeds (conserved[1]^2 + conserved[2]^2 + conserved[3]^2)/(2 conserved[0]) by at least 0.6; the speeds |conserved[m]/conserved[0]| stay below 1; conserved[5..7] lie between 0 and conserved[0].
All inputs are finite; a program needn't handle non-finite values.
Results may differ from a plain program's by a relative error of at most 0.0003.
Values sent between devices are 32-bit elements; how exact they have to be, the bound alone decides.
A program may use at most 64 MiB of HBM per device.

v0:
```python
import math

import jax
import jax.numpy as jnp
from jax import lax
from jax.sharding import PartitionSpec as P

ADIABATIC = 4.0 / 3.0
INNER_RADIUS = 1.0
OUTER_RADIUS = 2.0
COURANT = 0.4
GRAVITY_KICK = 0.004
MINIMUM_DENSITY = 0.05
PRESSURE_FLOOR = 0.01


def entering(part, axis, combine, identity):
    place = lax.axis_index(axis)
    gathered = lax.all_gather(part, axis)
    state = jnp.zeros_like(part) + jnp.asarray(identity, part.dtype)

    def one(lap, state):
        return combine(state, lax.dynamic_index_in_dim(gathered, lap, 0, False))

    return lax.fori_loop(0, place, one, state)


def extended_2(value, sides, width, wrap):
    for axis, dim in sides:
        peers, length = (lax.axis_size(axis), value.shape[dim])
        up = [(i, (i + 1) % peers) for i in range(peers if wrap else peers - 1)]
        down = [(j, i) for i, j in up]
        last = lax.slice_in_dim(value, length - width, length, axis=dim)
        initial = lax.slice_in_dim(value, 0, width, axis=dim)
        before = lax.ppermute(last, axis, up)
        after = lax.ppermute(initial, axis, down)
        value = jnp.concatenate([before, value, after], axis=dim)
    return value


def step_sizes(radial_total, phi_total, theta_total):
    theta_step = math.pi / theta_total
    phi_step = 2.0 * math.pi / phi_total
    polar_width = INNER_RADIUS * math.sin(0.5 * theta_step) * phi_step
    radial_step = min(2.0 * polar_width, (OUTER_RADIUS - INNER_RADIUS) / radial_total)
    timestep = COURANT * min(radial_step, polar_width)
    return (radial_step, theta_step, phi_step, timestep)


def thermo(values):
    density = jnp.maximum(values[0], MINIMUM_DENSITY)
    kinetic = (
        0.5 * (values[1] * values[1] + values[2] * values[2] + values[3] * values[3]) / density
    )
    pressure = jnp.maximum((ADIABATIC - 1.0) * (values[4] - kinetic), PRESSURE_FLOOR * density)
    return (density, pressure)


def physical(values, component):
    density, pressure = thermo(values)
    normal = values[component] / density
    sound = jnp.sqrt(ADIABATIC * pressure / density)
    pieces = [values[which] * normal for which in range(values.shape[0])]
    pieces[component] = pieces[component] + pressure
    pieces[4] = pieces[4] + pressure * normal
    return (jnp.stack(pieces), jnp.abs(normal) + sound)


def face_flux(values, along_dim, component):
    interior = values.shape[along_dim] - 4
    neighbour_differences = lax.slice_in_dim(
        values, 1, interior + 4, axis=along_dim
    ) - lax.slice_in_dim(values, 0, interior + 3, axis=along_dim)
    below_diff = lax.slice_in_dim(neighbour_differences, 0, interior + 2, axis=along_dim)
    above_diff = lax.slice_in_dim(neighbour_differences, 1, interior + 3, axis=along_dim)
    limited = (
        0.5
        * (jnp.sign(below_diff) + jnp.sign(above_diff))
        * jnp.minimum(jnp.abs(below_diff), jnp.abs(above_diff))
    )
    left_state = lax.slice_in_dim(values, 1, interior + 2, axis=along_dim) + 0.5 * lax.slice_in_dim(
        limited, 0, interior + 1, axis=along_dim
    )
    right_state = lax.slice_in_dim(
        values, 2, interior + 3, axis=along_dim
    ) - 0.5 * lax.slice_in_dim(limited, 1, interior + 2, axis=along_dim)
    left_flux, left_signal = physical(left_state, component)
    right_flux, right_signal = physical(right_state, component)
    signal = jnp.maximum(left_signal, right_signal)
    return 0.5 * (left_flux + right_flux) - 0.5 * signal * (right_state - left_state)


def hydro_rate(extended, cell_centers, enclosed, radial_step, theta_step, phi_step, strength):
    theta_cells = extended.shape[3]
    centre_cells = extended[:, 2:-2, 2:-2, :]
    polar_padded = jnp.pad(centre_cells, ((0, 0), (0, 0), (0, 0), (2, 2)), mode="edge")
    radial_flux = face_flux(extended[:, :, 2:-2, :], 1, 1)
    polar_flux = face_flux(polar_padded, 3, 2)
    azimuth_flux = face_flux(extended[:, 2:-2, :, :], 2, 3)
    angles = (jnp.arange(theta_cells, dtype=jnp.float32) + 0.5) * theta_step
    sine_center = jnp.sin(angles)
    cosine = jnp.cos(angles)
    face_sine = jnp.sin(jnp.arange(theta_cells + 1, dtype=jnp.float32) * theta_step)
    radius = cell_centers[:, None, None]
    face_radius = jnp.concatenate(
        [cell_centers - 0.5 * radial_step, cell_centers[-1:] + 0.5 * radial_step]
    )[:, None, None]
    radial_area = face_radius * face_radius * radial_flux
    divergence = (radial_area[:, 1:] - radial_area[:, :-1]) / (radius * radius * radial_step)
    polar_area = face_sine * polar_flux
    divergence = divergence + (polar_area[..., 1:] - polar_area[..., :-1]) / (
        radius * sine_center * theta_step
    )
    divergence = divergence + (azimuth_flux[:, :, 1:] - azimuth_flux[:, :, :-1]) / (
        radius * sine_center * phi_step
    )
    density, pressure = thermo(centre_cells)
    radial_speed = centre_cells[1] / density
    polar_speed = centre_cells[2] / density
    azimuth_speed = centre_cells[3] / density
    cotangent = cosine / sine_center
    gravity_pull = strength * enclosed[:, None, None] / (radius * radius)
    source_radial = (
        2.0 * pressure + density * (polar_speed * polar_speed + azimuth_speed * azimuth_speed)
    ) / radius - density * gravity_pull
    source_polar = (
        pressure * cotangent
        + density * azimuth_speed * azimuth_speed * cotangent
        - density * radial_speed * polar_speed
    ) / radius
    source_azimuth = -density * azimuth_speed * (radial_speed + polar_speed * cotangent) / radius
    source_energy = -centre_cells[1] * gravity_pull
    nothing = jnp.zeros_like(pressure)
    source = jnp.stack(
        [
            nothing,
            source_radial,
            source_polar,
            source_azimuth,
            source_energy,
            nothing,
            nothing,
            nothing,
        ]
    )
    return source - divergence


def add_terms(earlier, later):
    return earlier + later


def body(conserved, core_mass):
    radial_rows = conserved.shape[1]
    phi_cells = conserved.shape[2]
    theta_cells = conserved.shape[3]
    radial_devices = lax.axis_size("radial")
    position = lax.axis_index("radial")
    radial_step, theta_step, phi_step, timestep = step_sizes(
        radial_rows * radial_devices, phi_cells * lax.axis_size("phi"), theta_cells
    )
    strength = GRAVITY_KICK / timestep
    first_row = position * radial_rows
    cell_centers = (
        INNER_RADIUS
        + ((first_row + jnp.arange(radial_rows, dtype=jnp.int32)).astype(jnp.float32) + 0.5)
        * radial_step
    )
    sine_center = jnp.sin((jnp.arange(theta_cells, dtype=jnp.float32) + 0.5) * theta_step)
    local_shells = jnp.dot(
        jnp.sum(conserved[0], axis=1), sine_center, precision=lax.Precision.HIGHEST
    )
    local_shells = (
        local_shells * cell_centers * cell_centers * (radial_step * theta_step * phi_step)
    )
    shells = lax.psum(local_shells, "phi")
    before = entering(jnp.sum(shells), "radial", add_terms, jnp.float32(0.0))
    enclosed = core_mass[0] + before + jnp.cumsum(shells) - 0.5 * shells

    def clipped_rows(extended, halo_width):
        total_rows = extended.shape[1]
        low_rows = jnp.where(
            position == 0,
            lax.slice_in_dim(extended, halo_width, halo_width + 1, axis=1),
            lax.slice_in_dim(extended, 0, halo_width, axis=1),
        )
        high_rows = jnp.where(
            position == radial_devices - 1,
            lax.slice_in_dim(
                extended, total_rows - halo_width - 1, total_rows - halo_width, axis=1
            ),
            lax.slice_in_dim(extended, total_rows - halo_width, total_rows, axis=1),
        )
        middle = lax.slice_in_dim(extended, halo_width, total_rows - halo_width, axis=1)
        return jnp.concatenate([low_rows, middle, high_rows], axis=1)

    def extend(values):
        wedge_split_state = extended_2(values, (("phi", 2),), 2, True)
        slab_split_state = extended_2(wedge_split_state, (("radial", 1),), 2, False)
        return clipped_rows(slab_split_state, 2)

    section_one = conserved + timestep * hydro_rate(
        extend(conserved), cell_centers, enclosed, radial_step, theta_step, phi_step, strength
    )
    section_two = section_one + timestep * hydro_rate(
        extend(section_one), cell_centers, enclosed, radial_step, theta_step, phi_step, strength
    )
    advanced = 0.5 * conserved + 0.5 * section_two
    return (advanced, enclosed)


def solution(mesh):
    in_specs = (P(None, "radial", "phi", None), P())
    out_specs = (P(None, "radial", "phi", None), P("radial"))
    return jax.shard_map(body, mesh=mesh, in_specs=in_specs, out_specs=out_specs, check_vma=False)
```

profile of v0, /device:TPU:24, one launch (start us, length us, event | category | flops | bytes accessed | tf_op | source)
XLA Modules:
  0.0 98.6 jit_solution(16917580335347414988)
XLA Ops:
  0.6 1.1 %fusion.53 = (f32[8,8,2,128]{3,2,1,0:T(2,128)S(1)}, f32[8,8,2,128]{3,2,1,0:T(2,128)S(1)}) fusion(f32[8,8,16,128]{3,2,1,0:T(8,128)} %param.4), kind=kLoop, calls=%fused_computation.338 | loop fusion | bytes 262144 | tf_op jit(solution)/shard_map/slice | solution.py:33
  1.8 0.6 copy.673
  2.4 0.6 copy.674
  3.0 1.7 %collective-permute-start.1 = (f32[8,8,2,128]{3,1,2,0:T(8,128)}, f32[8,8,2,128]{3,1,2,0:T(8,128)}, u32[]{:S(2)}, u32[]{:S(2)}) collective-permute-start(f32[8,8,2,128]{3,1,2,0:T(8,128)} %copy.674), channel_id=1, source_target_pairs={{1,0},{2,1},{3,2},{0,3},{5,4},{6,5},{7,6},{4,7},{9,8},{10,9},{11,1... | collective-permute-start | bytes 196616 | tf_op jit(solution)/shard_map/ppermute | solution.py:36
  4.8 0.6 multiply_multiply_fusion.4
  5.3 0.5 broadcast_add_fusion
  6.2 0.7 fusion.44
  6.9 0.6 constant_dynamic-update-slice_fusion.61
  7.5 0.4 copy.675
  7.9 0.4 copy.676
  8.8 0.5 pad_maximum_fusion.6
  9.3 0.3 slice_subtract_fusion.1
  9.6 0.7 minimum_multiply_fusion.1
  10.4 0.8 fusion.6
  11.1 0.2 multiply_bitcast_fusion.1
  11.8 0.8 copy-done.1
  12.6 1.0 copy-done.3
  13.6 0.7 fusion.2
  14.3 5.8 %psum.7 = f32[8]{0:T(128)S(1)} all-reduce(f32[8]{0:T(128)} %fusion.2), channel_id=1, replica_groups=mesh['radial'=8,'phi'=4] {'phi'}, use_global_device_ids=true, to_apply=%region_1.0 | all-reduce | flops 8 | bytes 64 | tf_op jit(solution)/shard_map/psum | solution.py:176
  20.0 0.6 reduce_sum.19
  20.6 1.3 %dynamic-slice = u32[1]{0:T(128)} dynamic-slice(u32[32]{0:T(128)} %constant.10, u32[]{:T(128)S(6)} %add.633), dynamic_slice_sizes={1} | dynamic-slice | bytes 12
  21.9 0.5 broadcast.552
  22.4 2.4 %dynamic-update-slice = f32[8]{0:T(128)} dynamic-update-slice(f32[8]{0:T(128)} %broadcast.552, f32[1]{0:T(128)} %bitcast.4, u32[]{:T(128)} %bitcast.5) | dynamic-update-slice | bytes 12
  24.8 0.6 slice.710
  25.4 17.5 %all-reduce = f32[8]{0:T(128)} all-reduce(f32[8]{0:T(128)} %dynamic-update-slice), channel_id=1, replica_groups=mesh['radial'=8,'phi'=4] {'radial'}, use_global_device_ids=true, to_apply=%add | all-reduce | flops 8 | bytes 64
  42.9 11.3 %while.10 = (s32[]{:T(128)}, f32[]{:T(128)}, s32[]{:T(128)}, f32[8]{0:T(128)}, s32[]{:T(128)}, /*index=5*/s32[]{:T(128)}, s32[]{:T(128)}) while((s32[]{:T(128)}, f32[]{:T(128)}, s32[]{:T(128)}, f32[8]{0:T(128)}, s32[]{:T(128)}, /*index=5*/s32[]{:T(128)}, s32[]{:T(128)}) %tuple.74), condition=%wide.region_4.5_spmd, body=%wide.region_3.4_spmd.sunk | while | flops 6 | bytes 135 | solution.py:25
  42.9 1.2 %dynamic_slice.5 = f32[1]{0:T(128)} dynamic-slice(f32[8]{0:T(128)} %get-tuple-element.163, s32[]{:T(128)S(6)} %select_n.41), dynamic_slice_sizes={1} | dynamic-slice | bytes 12 | tf_op jit(solution)/shard_map/while/body/jit(dynamic_index_in_dim)/dynamic_slice | solution.py:23
  44.8 1.2 %dynamic_slice.5 = f32[1]{0:T(128)} dynamic-slice(f32[8]{0:T(128)} %get-tuple-element.163, s32[]{:T(128)S(6)} %select_n.41), dynamic_slice_sizes={1} | dynamic-slice | bytes 12 | tf_op jit(solution)/shard_map/while/body/jit(dynamic_index_in_dim)/dynamic_slice | solution.py:23
  46.6 1.2 %dynamic_slice.5 = f32[1]{0:T(128)} dynamic-slice(f32[8]{0:T(128)} %get-tuple-element.163, s32[]{:T(128)S(6)} %select_n.41), dynamic_slice_sizes={1} | dynamic-slice | bytes 12 | tf_op jit(solution)/shard_map/while/body/jit(dynamic_index_in_dim)/dynamic_slice | solution.py:23
  48.5 1.2 %dynamic_slice.5 = f32[1]{0:T(128)} dynamic-slice(f32[8]{0:T(128)} %get-tuple-element.163, s32[]{:T(128)S(6)} %select_n.41), dynamic_slice_sizes={1} | dynamic-slice | bytes 12 | tf_op jit(solution)/shard_map/while/body/jit(dynamic_index_in_dim)/dynamic_slice | solution.py:23
  50.4 1.2 %dynamic_slice.5 = f32[1]{0:T(128)} dynamic-slice(f32[8]{0:T(128)} %get-tuple-element.163, s32[]{:T(128)S(6)} %select_n.41), dynamic_slice_sizes={1} | dynamic-slice | bytes 12 | tf_op jit(solution)/shard_map/while/body/jit(dynamic_index_in_dim)/dynamic_slice | solution.py:23
  52.3 1.2 %dynamic_slice.5 = f32[1]{0:T(128)} dynamic-slice(f32[8]{0:T(128)} %get-tuple-element.163, s32[]{:T(128)S(6)} %select_n.41), dynamic_slice_sizes={1} | dynamic-slice | bytes 12 | tf_op jit(solution)/shard_map/while/body/jit(dynamic_index_in_dim)/dynamic_slice | solution.py:23
  54.8 0.7 reduce-window.9
  55.5 1.2 %multiply_divide_fusion = (f32[8]{0:T(128)S(1)}, f32[8]{0:T(128)}) fusion(s32[]{:T(128)S(6)} %mul.1524, f32[8]{0:T(128)S(1)} %psum.7, f32[8,1]{0,1:T(1,128)} %reduce-window.9, f32[]{:T(128)S(6)} %add.521), kind=kLoop, calls=%fused_computation.325 | loop fusion | flops 88 | bytes 136 | tf_op jit(solution)/shard_map/div | solution.py:122
  57.1 0.8 multiply_multiply_fusion.3
  58.5 0.7 constant_dynamic-update-slice_fusion.23
  59.2 1.8 %subtract_multiply_fusion.1 = f32[8,8,16,129]{3,2,1,0:T(8,128)S(1)} fusion(f32[8,8,16,129]{3,2,1,0:T(8,128)S(1)} %get-tuple-element.87, f32[8,8,16,129]{3,2,1,0:T(8,128)S(1)} %get-tuple-element.86, f32[8,8,16,129]{3,2,1,0:T(8,128)} %get-tuple-element.116, f32[8,8,16,129]{3,2,1,0:T(8,128)S(1)} %get-tuple-element.117, f32[8,16,129]{2,1,0:T(8,128)S(1)} %get-tuple-element.70, ...), kind=kLoop, calls=%fused_computation.24 | loop fusion | flops 792576 | bytes 2708484 | tf_op jit(solution)/shard_map/mul | solution.py:110
  61.0 0.9 copy.630
  61.9 0.9 copy.631
  63.1 1.9 %collective-permute-start.3 = (f32[8,2,20,128]{3,0,2,1:T(8,128)S(1)}, f32[8,2,20,128]{3,0,2,1:T(8,128)S(1)}, u32[]{:S(2)}, u32[]{:S(2)}) collective-permute-start(f32[8,2,20,128]{3,0,2,1:T(8,128)S(1)} %copy.638), channel_id=1, source_target_pairs={{4,0},{8,4},{12,8},{16,12},{20,16},{24,20},{28,24},{5,1},{9,5},{13... | collective-permute-start | bytes 491528 | tf_op jit(solution)/shard_map/ppermute | solution.py:36
  65.1 4.7 %collective-permute-start.2 = (f32[8,2,20,128]{3,0,2,1:T(8,128)S(1)}, f32[8,2,20,128]{3,0,2,1:T(8,128)S(1)}, u32[]{:S(2)}, u32[]{:S(2)}) collective-permute-start(f32[8,2,20,128]{3,0,2,1:T(8,128)S(1)} %copy.634), channel_id=1, source_target_pairs={{0,4},{4,8},{8,12},{12,16},{16,20},{20,24},{24,28},{1,5},{5,9},{9,... | collective-permute-start | bytes 491528 | tf_op jit(solution)/shard_map/ppermute | solution.py:35
  69.8 0.6 minimum_multiply_fusion.3
  70.4 0.3 fusion.10
  71.6 1.6 %collective-permute-done.2 = f32[8,2,20,128]{3,0,2,1:T(8,128)S(1)} collective-permute-done((f32[8,2,20,128]{3,0,2,1:T(8,128)S(1)}, f32[8,2,20,128]{3,0,2,1:T(8,128)S(1)}, u32[]{:S(2)}, u32[]{:S(2)}) %collective-permute-start.2) | collective-permute-done | bytes 163872 | tf_op jit(solution)/shard_map/ppermute | solution.py:35
  73.5 0.3 minimum_multiply_fusion.5
  74.6 0.5 copy-done.5
  75.0 0.4 fusion.28
  75.5 0.5 slice_reduce_fusion.1
  76.1 1.7 %collective-permute-start.5 = (f32[8,8,2,128]{3,1,2,0:T(8,128)S(1)}, f32[8,8,2,128]{3,1,2,0:T(8,128)S(1)}, u32[]{:S(2)}, u32[]{:S(2)}) collective-permute-start(f32[8,8,2,128]{3,1,2,0:T(8,128)S(1)} %copy.649), channel_id=1, source_target_pairs={{1,0},{2,1},{3,2},{0,3},{5,4},{6,5},{7,6},{4,7},{9,8},{10,9},{11,1... | collective-permute-start | bytes 196616 | tf_op jit(solution)/shard_map/ppermute | solution.py:36
  78.2 0.5 pad_maximum_fusion.7
  78.7 0.3 slice_subtract_fusion
  79.0 0.7 minimum_multiply_fusion
  79.8 0.8 fusion.4
  80.5 0.2 multiply_bitcast_fusion
  81.3 0.9 copy-done.4
  82.5 0.5 subtract_multiply_fusion
  83.5 3.8 %collective-permute-start.6 = (f32[8,2,20,128]{3,0,2,1:T(8,128)S(1)}, f32[8,2,20,128]{3,0,2,1:T(8,128)S(1)}, u32[]{:S(2)}, u32[]{:S(2)}) collective-permute-start(f32[8,2,20,128]{3,0,2,1:T(8,128)S(1)} %copy.654), channel_id=1, source_target_pairs={{0,4},{4,8},{8,12},{12,16},{16,20},{20,24},{24,28},{1,5},{5,9},{9,... | collective-permute-start | bytes 491528 | tf_op jit(solution)/shard_map/ppermute | solution.py:35
  87.4 2.9 %collective-permute-start.7 = (f32[8,2,20,128]{3,0,2,1:T(8,128)S(1)}, f32[8,2,20,128]{3,0,2,1:T(8,128)S(1)}, u32[]{:S(2)}, u32[]{:S(2)}) collective-permute-start(f32[8,2,20,128]{3,0,2,1:T(8,128)S(1)} %copy.658), channel_id=1, source_target_pairs={{4,0},{8,4},{12,8},{16,12},{20,16},{24,20},{28,24},{5,1},{9,5},{13... | collective-permute-start | bytes 491528 | tf_op jit(solution)/shard_map/ppermute | solution.py:36
  90.3 0.6 minimum_multiply_fusion.2
  90.9 0.3 fusion.8
  92.0 0.6 collective-permute-done.6
  92.6 3.4 %collective-permute-done.7 = f32[8,2,20,128]{3,0,2,1:T(8,128)S(1)} collective-permute-done((f32[8,2,20,128]{3,0,2,1:T(8,128)S(1)}, f32[8,2,20,128]{3,0,2,1:T(8,128)S(1)}, u32[]{:S(2)}, u32[]{:S(2)}) %collective-permute-start.7) | collective-permute-done | bytes 163872 | tf_op jit(solution)/shard_map/ppermute | solution.py:36
  96.3 0.3 minimum_multiply_fusion.4
  97.4 1.2 %fusion.32 = f32[8,8,16,128]{3,2,1,0:T(8,128)} fusion(f32[8,8,16,128]{3,2,1,0:T(8,128)S(1)} %copy-done, f32[8,8,16,128]{3,2,1,0:T(8,128)S(1)} %fusion.28, f32[8,8,16,128]{3,2,1,0:T(8,128)S(1)} %constant_dynamic-update-slice_fusion.55, f32[8,8,17,128]{3,2,1,0:T(8,128)S(1)} %multiply_subtract_fusion, f32[8,8,16,129]{3,2,1,0:T(8,128)S(1)} %subtract_multiply_fusion, ...), kind=kLoop, calls=%fused_computation.97 | loop fusion | flops 1703936 | bytes 5251104 | tf_op jit(solution)/shard_map/add | solution.py:208
  (166 shorter events, 6.9 us)
Async XLA Ops:
  0.6 5.2 %copy-start = (f32[8,8,16,128]{3,2,1,0:T(8,128)S(1)}, f32[8,8,16,128]{3,2,1,0:T(8,128)}, u32[]{:S(2)}) copy-start(f32[8,8,16,128]{3,2,1,0:T(8,128)} %param.4) | copy-start | bytes 1572868
  2.4 58.6 %collective-permute-start = (f32[8,8,2,128]{3,1,2,0:T(8,128)}, f32[8,8,2,128]{3,1,2,0:T(8,128)}, u32[]{:S(2)}, u32[]{:S(2)}) collective-permute-start(f32[8,8,2,128]{3,1,2,0:T(8,128)} %copy.673), channel_id=1, source_target_pairs={{0,1},{1,2},{2,3},{3,0},{4,5},{5,6},{6,7},{7,4},{8,9},{9,10},{10,1... | collective-permute-start | bytes 196616 | tf_op jit(solution)/shard_map/ppermute | solution.py:35
  3.0 58.9 %collective-permute-start.1 = (f32[8,8,2,128]{3,1,2,0:T(8,128)}, f32[8,8,2,128]{3,1,2,0:T(8,128)}, u32[]{:S(2)}, u32[]{:S(2)}) collective-permute-start(f32[8,8,2,128]{3,1,2,0:T(8,128)} %copy.674), channel_id=1, source_target_pairs={{1,0},{2,1},{3,2},{0,3},{5,4},{6,5},{7,6},{4,7},{9,8},{10,9},{11,1... | collective-permute-start | bytes 196616 | tf_op jit(solution)/shard_map/ppermute | solution.py:36
  11.6 1.0 copy-start.1
  12.6 1.0 %copy-start.3 = (f32[8,8,16,129]{3,2,1,0:T(8,128)}, f32[8,8,16,129]{3,2,1,0:T(8,128)S(1)}, u32[]{:S(2)}) copy-start(f32[8,8,16,129]{3,2,1,0:T(8,128)S(1)} %constant_dynamic-update-slice_fusion.24) | copy-start | bytes 1585156
  55.5 3.0 %copy-start.2 = (f32[8,8,16,129]{3,2,1,0:T(8,128)S(1)}, f32[8,8,16,129]{3,2,1,0:T(8,128)}, u32[]{:S(2)}) copy-start(f32[8,8,16,129]{3,2,1,0:T(8,128)} %copy-done.1) | copy-start | bytes 1585156
  59.2 1.8 %copy-start.6 = (f32[8]{0:T(128)S(1)}, f32[8]{0:T(128)}, u32[]{:S(2)}) copy-start(f32[8]{0:T(128)} %broadcast_add_fusion) | copy-start | bytes 100
  63.1 8.4 %collective-permute-start.3 = (f32[8,2,20,128]{3,0,2,1:T(8,128)S(1)}, f32[8,2,20,128]{3,0,2,1:T(8,128)S(1)}, u32[]{:S(2)}, u32[]{:S(2)}) collective-permute-start(f32[8,2,20,128]{3,0,2,1:T(8,128)S(1)} %copy.638), channel_id=1, source_target_pairs={{4,0},{8,4},{12,8},{16,12},{20,16},{24,20},{28,24},{5,1},{9,5},{13... | collective-permute-start | bytes 491528 | tf_op jit(solution)/shard_map/ppermute | solution.py:36
  65.1 8.1 %collective-permute-start.2 = (f32[8,2,20,128]{3,0,2,1:T(8,128)S(1)}, f32[8,2,20,128]{3,0,2,1:T(8,128)S(1)}, u32[]{:S(2)}, u32[]{:S(2)}) collective-permute-start(f32[8,2,20,128]{3,0,2,1:T(8,128)S(1)} %copy.634), channel_id=1, source_target_pairs={{0,4},{4,8},{8,12},{12,16},{16,20},{20,24},{24,28},{1,5},{5,9},{9,... | collective-permute-start | bytes 491528 | tf_op jit(solution)/shard_map/ppermute | solution.py:35
  74.4 0.7 copy-start.5
  76.0 7.1 %collective-permute-start.4 = (f32[8,8,2,128]{3,1,2,0:T(8,128)S(1)}, f32[8,8,2,128]{3,1,2,0:T(8,128)S(1)}, u32[]{:S(2)}, u32[]{:S(2)}) collective-permute-start(f32[8,8,2,128]{3,1,2,0:T(8,128)S(1)} %copy.648), channel_id=1, source_target_pairs={{0,1},{1,2},{2,3},{3,0},{4,5},{5,6},{6,7},{7,4},{8,9},{9,10},{10,1... | collective-permute-start | bytes 196616 | tf_op jit(solution)/shard_map/ppermute | solution.py:35
  76.1 7.0 %collective-permute-start.5 = (f32[8,8,2,128]{3,1,2,0:T(8,128)S(1)}, f32[8,8,2,128]{3,1,2,0:T(8,128)S(1)}, u32[]{:S(2)}, u32[]{:S(2)}) collective-permute-start(f32[8,8,2,128]{3,1,2,0:T(8,128)S(1)} %copy.649), channel_id=1, source_target_pairs={{1,0},{2,1},{3,2},{0,3},{5,4},{6,5},{7,6},{4,7},{9,8},{10,9},{11,1... | collective-permute-start | bytes 196616 | tf_op jit(solution)/shard_map/ppermute | solution.py:36
  81.1 1.0 %copy-start.4 = (f32[8,8,16,128]{3,2,1,0:T(8,128)S(1)}, f32[8,8,16,128]{3,2,1,0:T(8,128)}, u32[]{:S(2)}) copy-start(f32[8,8,16,128]{3,2,1,0:T(8,128)} %constant_dynamic-update-slice_fusion.61) | copy-start | bytes 1572868
  83.5 9.1 %collective-permute-start.6 = (f32[8,2,20,128]{3,0,2,1:T(8,128)S(1)}, f32[8,2,20,128]{3,0,2,1:T(8,128)S(1)}, u32[]{:S(2)}, u32[]{:S(2)}) collective-permute-start(f32[8,2,20,128]{3,0,2,1:T(8,128)S(1)} %copy.654), channel_id=1, source_target_pairs={{0,4},{4,8},{8,12},{12,16},{16,20},{20,24},{24,28},{1,5},{5,9},{9,... | collective-permute-start | bytes 491528 | tf_op jit(solution)/shard_map/ppermute | solution.py:35
  87.4 8.6 %collective-permute-start.7 = (f32[8,2,20,128]{3,0,2,1:T(8,128)S(1)}, f32[8,2,20,128]{3,0,2,1:T(8,128)S(1)}, u32[]{:S(2)}, u32[]{:S(2)}) collective-permute-start(f32[8,2,20,128]{3,0,2,1:T(8,128)S(1)} %copy.658), channel_id=1, source_target_pairs={{4,0},{8,4},{12,8},{16,12},{20,16},{24,20},{28,24},{5,1},{9,5},{13... | collective-permute-start | bytes 491528 | tf_op jit(solution)/shard_map/ppermute | solution.py:36
where the time goes:
time: 99.2 us; the launch traced here: 98.6 us
  blocking collectives  23.2 us (23%)
  local copies, waits for them, and re-layouts  22.9 us (23%)
  other arithmetic  22.4 us (23%)
  starting transfers between devices  16.9 us (17%)
  waiting for transfers between devices  5.66 us (6%)
  loops' own time  3.87 us (4%)
  between operations  3 us (3%)
    unnamed x1, blocking collectives  17.5 us
    unnamed x25, local copies, waits for them, and re-layouts  10.1 us
    ppermute x4, starting transfers between devices, extended_2(): before = lax.ppermute(last, axis, up)  8.58 us
    ppermute x4, starting transfers between devices, extended_2(): after = lax.ppermute(initial, axis, down)  8.32 us
    dynamic_slice x6, local copies, waits for them, and re-layouts, one(): return combine(state, lax.dynamic_index_in_dim(gathered, lap, 0, False))  7.39 us
    psum x1, blocking collectives, body(): shells = lax.psum(local_shells, 'phi')  5.76 us
    another operation x1, loops' own time, entering(): return lax.fori_loop(0, place, one, state)  3.87 us
    ppermute x4, waiting for transfers between devices, extended_2(): after = lax.ppermute(initial, axis, down)  3.39 us
  transfers between devices with their start and end apart: 8, of which 3 were waited for; matrix products, arithmetic and copies ran while one was open for 35% of the time, Pallas kernels for 0%

commit v1 on v0

v1 whole, which is shorter than its diff:
```python
import functools
import math

import jax
import jax.numpy as jnp
import numpy as np
from jax import lax
from jax.experimental import pallas as pl
from jax.experimental.pallas import tpu as pltpu
from jax.sharding import PartitionSpec as P

ADIABATIC = 4.0 / 3.0
INNER_RADIUS = 1.0
OUTER_RADIUS = 2.0
COURANT = 0.4
GRAVITY_KICK = 0.004
MINIMUM_DENSITY = 0.05
PRESSURE_FLOOR = 0.01
MESH = pl.DeviceIdType.MESH
TILE = 8
PAD = 8


def step_sizes(radial_total, phi_total, theta_total):
    theta_step = math.pi / theta_total
    phi_step = 2.0 * math.pi / phi_total
    polar_width = INNER_RADIUS * math.sin(0.5 * theta_step) * phi_step
    radial_step = min(2.0 * polar_width, (OUTER_RADIUS - INNER_RADIUS) / radial_total)
    timestep = COURANT * min(radial_step, polar_width)
    return (radial_step, theta_step, phi_step, timestep)


def angle_tables(theta_cells, theta_step):
    step = np.float32(theta_step)
    centre = (np.arange(theta_cells, dtype=np.float32) + np.float32(0.5)) * step
    face = np.arange(theta_cells + 1, dtype=np.float32) * step
    sine = np.sin(centre.astype(np.float64))
    cosine = np.cos(centre.astype(np.float64))
    face_sine = np.sin(face.astype(np.float64))
    zero = np.zeros(theta_cells)
    rows = [sine, face_sine[:-1], face_sine[1:], cosine / sine, 1.0 / sine, zero, zero, zero]
    return np.stack(rows).astype(np.float32)


def half_slope(below, above):
    return 0.5 * (
        jnp.maximum(jnp.minimum(below, above), 0.0) + jnp.minimum(jnp.maximum(below, above), 0.0)
    )


def thermo(q):
    density = jnp.maximum(q[0], MINIMUM_DENSITY)
    inverse = 1.0 / density
    kinetic = 0.5 * (q[1] * q[1] + q[2] * q[2] + q[3] * q[3]) * inverse
    pressure = jnp.maximum((ADIABATIC - 1.0) * (q[4] - kinetic), PRESSURE_FLOOR * density)
    return density, inverse, pressure


def physical(q, component):
    _, inverse, pressure = thermo(q)
    normal = q[component] * inverse
    squared = ADIABATIC * pressure * inverse
    return normal, pressure, jnp.abs(normal) + squared * lax.rsqrt(squared)


def flux(left, right, component):
    left_v, left_p, left_a = physical(left, component)
    right_v, right_p, right_a = physical(right, component)
    signal = jnp.maximum(left_a, right_a)
    left_w = 0.5 * (left_v + signal)
    right_w = 0.5 * (right_v - signal)
    out = [a * left_w + b * right_w for a, b in zip(left, right)]
    out[component] = out[component] + 0.5 * (left_p + right_p)
    out[4] = out[4] + 0.5 * (left_p * left_v + right_p * right_v)
    return out


def two_faces(rows, component):
    lower_left, lower_right, upper_left, upper_right = [], [], [], []
    for a, b, c, d, e in zip(*rows):
        ab, bc, cd, de = b - a, c - b, d - c, e - d
        sb, sc, sd = half_slope(ab, bc), half_slope(bc, cd), half_slope(cd, de)
        lower_left.append(b + sb)
        lower_right.append(c - sc)
        upper_left.append(c + sc)
        upper_right.append(d - sd)
    return flux(lower_left, lower_right, component), flux(upper_left, upper_right, component)


def kernel(
    sizes,
    counts,
    core_ref,
    table_ref,
    input_ref,
    out_ref,
    mass_ref,
    first,
    second,
    edge,
    halo,
    phi_part,
    phi_got,
    slab_part,
    slab_got,
    pull,
    load_sem,
    radial_send,
    radial_recv,
    phi_send,
    phi_recv,
    part_send,
    part_recv,
    slab_send,
    slab_recv,
):
    radial_step, theta_step, phi_step, timestep = sizes
    slabs, wedges = counts
    variables, rows, cells, lanes = input_ref.shape
    tiles = cells // TILE
    strength = GRAVITY_KICK / timestep
    slab, wedge = lax.axis_index("radial"), lax.axis_index("phi")
    has_up, has_down = slab < slabs - 1, slab > 0

    load = pltpu.make_async_copy(
        input_ref, first.at[:, pl.ds(2, rows), pl.ds(PAD, cells), :], load_sem
    )
    load.start()

    def radial_peer(jump):
        return (lax.rem(slab + jump, slabs), wedge)

    def phi_peer(jump):
        return (slab, lax.rem(wedge + jump, wedges))

    barrier = pltpu.get_barrier_semaphore()
    peers = [radial_peer(j) for j in range(1, slabs)] + [phi_peer(j) for j in range(1, wedges)]
    for peer in peers:
        pl.semaphore_signal(barrier, inc=1, device_id=peer, device_id_type=MESH)
    pl.semaphore_wait(barrier, len(peers))
    load.wait()

    def remote(src, dst, send, recv, peer):
        return pltpu.make_async_remote_copy(
            src_ref=src, dst_ref=dst, send_sem=send, recv_sem=recv, device_id=peer,
            device_id_type=MESH,
        )

    def radial_copies(buffer, section, tile):
        where = pl.ds(PAD + TILE * tile, TILE)
        slot = (section * tiles + tile) * 2
        up = remote(
            buffer.at[:, pl.ds(rows, 2), where, :], buffer.at[:, pl.ds(0, 2), where, :],
            radial_send.at[slot], radial_recv.at[slot], radial_peer(1),
        )
        down = remote(
            buffer.at[:, pl.ds(2, 2), where, :], buffer.at[:, pl.ds(rows + 2, 2), where, :],
            radial_send.at[slot + 1], radial_recv.at[slot + 1], radial_peer(slabs - 1),
        )
        return up, down

    def radial_start(copies):
        up, down = copies

        @pl.when(has_up)
        def _():
            up.start()

        @pl.when(has_down)
        def _():
            down.start()

    def radial_sent(copies):
        up, down = copies

        @pl.when(has_up)
        def _():
            up.wait_send()

        @pl.when(has_down)
        def _():
            down.wait_send()

    def radial_land(copies, buffer, tile):
        up, down = copies
        where = pl.ds(PAD + TILE * tile, TILE)

        @pl.when(has_down)
        def _():
            up.wait_recv()

        @pl.when(jnp.logical_not(has_down))
        def _():
            value = buffer[:, 2, where, :]
            buffer[:, 0, where, :] = value
            buffer[:, 1, where, :] = value

        @pl.when(has_up)
        def _():
            down.wait_recv()

        @pl.when(jnp.logical_not(has_up))
        def _():
            value = buffer[:, rows + 1, where, :]
            buffer[:, rows + 2, where, :] = value
            buffer[:, rows + 3, where, :] = value

    def phi_copies(section):
        slot = section * 2
        return [
            remote(
                edge.at[slot + side], halo.at[slot + side], phi_send.at[slot + side],
                phi_recv.at[slot + side], phi_peer(jump),
            )
            for side, jump in ((0, wedges - 1), (1, 1))
        ]

    def phi_pack(buffer, section, side):
        start = PAD if side == 0 else PAD + cells - 2
        edge[section * 2 + side] = buffer[:, pl.ds(2, rows), pl.ds(start, 2), :]

    def phi_unpack(buffer, section, side):
        start = PAD + cells if side == 0 else PAD - 2
        buffer[:, pl.ds(2, rows), pl.ds(start, 2), :] = halo[section * 2 + side]

    shape = (TILE, lanes)
    lane = lax.broadcasted_iota(jnp.int32, (rows, lanes), 1)
    line = lax.broadcasted_iota(jnp.int32, (rows, lanes), 0)
    column = jnp.sum(first[0, pl.ds(2, rows), pl.ds(PAD, cells), :], axis=1)
    column = jnp.sum(column * table_ref[0:1, :], axis=1, keepdims=True)
    centres = INNER_RADIUS + (
        (slab * rows + line).astype(jnp.float32) + 0.5
    ) * radial_step
    column = column * centres * centres * (radial_step * theta_step * phi_step)
    phi_part[...] = jnp.sum(jnp.where(lane == line, column, 0.0), axis=0, keepdims=True)
    part_copies = [
        remote(phi_part, phi_got.at[j], part_send.at[j], part_recv.at[j], phi_peer(j))
        for j in range(1, wedges)
    ]
    for copy in part_copies:
        copy.start()
    first_radial = [radial_copies(first, 0, t) for t in range(tiles)]
    second_radial = [radial_copies(second, 1, t) for t in range(tiles)]
    radial_start(first_radial[0])
    phi_pack(first, 0, 0)
    phi_pack(first, 0, 1)
    first_phi, second_phi = phi_copies(0), phi_copies(1)
    for copy in first_phi:
        copy.start()

    total = phi_part[...]
    for j, copy in enumerate(part_copies, 1):
        copy.wait_recv()
        total = total + phi_got[j]
    slab_part[...] = total
    slab_copies = [
        remote(slab_part, slab_got.at[j], slab_send.at[j], slab_recv.at[j], radial_peer(j))
        for j in range(1, slabs)
    ]
    for copy in slab_copies:
        copy.start()
    for t in range(1, tiles):
        radial_start(first_radial[t])

    lane_tile = lax.broadcasted_iota(jnp.int32, shape, 1)
    is_first, is_last = lane_tile == 0, lane_tile == lanes - 1

    def rate(buffer, r, tile):
        start = PAD + TILE * tile

        def at(row, offset):
            return [buffer[k, row + 2, pl.ds(start + offset, TILE), :] for k in range(variables)]

        def spread(value):
            return jnp.broadcast_to(value, shape)

        index = jnp.full(shape, slab * rows + r, jnp.int32).astype(jnp.float32)
        radius = INNER_RADIUS + (index + 0.5) * radial_step
        inner, outer = radius - 0.5 * radial_step, radius + 0.5 * radial_step
        inverse_r = 1.0 / radius
        centre = at(r, 0)
        lower, upper = two_faces([at(r + o, 0) if o else centre for o in range(-2, 3)], 1)
        scale = inverse_r * inverse_r * (1.0 / radial_step)
        area_in, area_out = inner * inner * scale, outer * outer * scale
        total = [area_in * a - area_out * b for a, b in zip(lower, upper)]
        lower, upper = two_faces([at(r, o) if o else centre for o in range(-2, 3)], 3)
        around = inverse_r * spread(table_ref[4:5, :])
        scale = around * (1.0 / phi_step)
        total = [t + (a - b) * scale for t, a, b in zip(total, lower, upper)]
        left, right = [], []
        for q in centre:
            after = jnp.where(is_last, q, pltpu.roll(q, lanes - 1, 1))
            above = after - q
            below = jnp.where(is_first, 0.0, pltpu.roll(above, 1, 1))
            slope = half_slope(below, above)
            left.append(q + slope)
            right.append(jnp.where(is_last, q, pltpu.roll(q - slope, lanes - 1, 1)))
        upper = flux(left, right, 2)
        scale = around * (1.0 / theta_step)
        low_sine, high_sine = spread(table_ref[1:2, :]), spread(table_ref[2:3, :])
        low_area, high_area = low_sine * scale, high_sine * scale
        total = [
            t + (low_area * pltpu.roll(f, 1, 1) - high_area * f) for t, f in zip(total, upper)
        ]
        density, inverse, pressure = thermo(centre)
        vr, vt, vp = (centre[m] * inverse for m in (1, 2, 3))
        cot = spread(table_ref[3:4, :])
        total[1] = total[1] + (2.0 * pressure + density * (vt * vt + vp * vp)) * inverse_r
        total[2] = total[2] + (
            (pressure + density * vp * vp) * cot - density * vr * vt
        ) * inverse_r
        total[3] = total[3] - density * vp * (vr + vt * cot) * inverse_r
        return centre, density, total, inverse_r

    def gravity_at(r):
        return jnp.broadcast_to(pull[pl.ds(r, 1), :], shape)

    def section_one(r, tile, with_gravity):
        centre, density, total, _ = rate(first, r, tile)
        if with_gravity:
            gravity = gravity_at(r)
            total[1] = total[1] - density * gravity
            total[4] = total[4] - centre[1] * gravity
        where = pl.ds(PAD + TILE * tile, TILE)
        for k in range(variables):
            second[k, r + 2, where, :] = centre[k] + timestep * total[k]

    def late_gravity(r, tile):
        where = pl.ds(PAD + TILE * tile, TILE)
        gravity = timestep * gravity_at(r)
        density = jnp.maximum(first[0, r + 2, where, :], MINIMUM_DENSITY)
        second[1, r + 2, where, :] = second[1, r + 2, where, :] - density * gravity
        second[4, r + 2, where, :] = (
            second[4, r + 2, where, :] - first[1, r + 2, where, :] * gravity
        )

    def section_two(r, tile):
        centre, density, total, _ = rate(second, r, tile)
        gravity = gravity_at(r)
        total[1] = total[1] - density * gravity
        total[4] = total[4] - centre[1] * gravity
        where = pl.ds(PAD + TILE * tile, TILE)
        into = pl.ds(TILE * tile, TILE)
        for k in range(variables):
            begin = first[k, r + 2, where, :]
            out_ref[k, r, into, :] = 0.5 * begin + 0.5 * (centre[k] + timestep * total[k])

    def each_row(low, high, step):
        lax.fori_loop(low, high, lambda r, _: (step(r), 0)[1], 0)

    def each_edge(step):
        lax.fori_loop(
            0, 4, lambda i, _: (step(i + (i // 2) * (rows - 4)), 0)[1], 0
        )

    def all_tiles(step):
        def run(r):
            for t in range(tiles):
                step(r, t)

        return run

    for side, copy in enumerate(first_phi):
        copy.wait_recv()
        phi_unpack(first, 0, side)
    each_row(2, rows - 2, all_tiles(lambda r, t: section_one(r, t, False)))

    before = jnp.zeros((1, lanes), jnp.float32)
    for j, copy in enumerate(slab_copies, 1):
        copy.wait_recv()
        before = before + jnp.where(slab >= j, slab_got[j], 0.0)
    before = jnp.sum(before, axis=1, keepdims=True)
    weight = jnp.where(lane < line, 1.0, jnp.where(lane == line, 0.5, 0.0))
    within = jnp.sum(weight * slab_part[...], axis=1, keepdims=True)
    enclosed = core_ref[0] + before + within + jnp.zeros((rows, lanes), jnp.float32)
    mass_ref[...] = jnp.sum(jnp.where(lane == line, enclosed, 0.0), axis=0, keepdims=True)[:, :rows]
    pull[...] = strength * enclosed / (centres * centres)
    each_row(2, rows - 2, all_tiles(late_gravity))

    for t in range(tiles):
        radial_land(first_radial[t], first, t)
        each_edge(lambda r: section_one(r, t, True))
        radial_start(second_radial[t])
        if t == 0:
            phi_pack(second, 1, 0)
            second_phi[0].start()
        if t == tiles - 1:
            phi_pack(second, 1, 1)
            second_phi[1].start()
    for side, copy in enumerate(second_phi):
        copy.wait_recv()
        phi_unpack(second, 1, side)
    each_row(2, rows - 2, all_tiles(section_two))
    for t in range(tiles):
        radial_land(second_radial[t], second, t)
        each_edge(lambda r: section_two(r, t))

    for copy in part_copies + slab_copies + first_phi + second_phi:
        copy.wait_send()
    for copies in first_radial + second_radial:
        radial_sent(copies)


def body(conserved, core_mass):
    variables, rows, cells, lanes = conserved.shape
    slabs, wedges = lax.axis_size("radial"), lax.axis_size("phi")
    sizes = step_sizes(rows * slabs, cells * wedges, lanes)
    table = jnp.asarray(angle_tables(lanes, sizes[1]))
    tiles = cells // TILE
    padded = (variables, rows + 4, cells + 2 * PAD, lanes)
    vmem = pl.BlockSpec(memory_space=pltpu.VMEM)
    dma = pltpu.SemaphoreType.DMA
    advanced, mass = pl.pallas_call(
        functools.partial(kernel, sizes, (slabs, wedges)),
        out_shape=(
            jax.ShapeDtypeStruct(conserved.shape, jnp.float32),
            jax.ShapeDtypeStruct((1, rows), jnp.float32),
        ),
        in_specs=[
            pl.BlockSpec(memory_space=pltpu.SMEM), vmem, pl.BlockSpec(memory_space=pl.ANY),
        ],
        out_specs=(vmem, vmem),
        scratch_shapes=[
            pltpu.VMEM(padded, jnp.float32),
            pltpu.VMEM(padded, jnp.float32),
            pltpu.VMEM((4, variables, rows, 2, lanes), jnp.float32),
            pltpu.VMEM((4, variables, rows, 2, lanes), jnp.float32),
            pltpu.VMEM((1, lanes), jnp.float32),
            pltpu.VMEM((wedges, 1, lanes), jnp.float32),
            pltpu.VMEM((1, lanes), jnp.float32),
            pltpu.VMEM((slabs, 1, lanes), jnp.float32),
            pltpu.VMEM((rows, lanes), jnp.float32),
            dma,
            dma((4 * tiles,)),
            dma((4 * tiles,)),
            dma((4,)),
            dma((4,)),
            dma((wedges,)),
            dma((wedges,)),
            dma((slabs,)),
            dma((slabs,)),
        ],
        compiler_params=pltpu.CompilerParams(collective_id=0, has_side_effects=True),
    )(core_mass, table, conserved)
    return advanced, mass.reshape(rows)


def solution(mesh):
    in_specs = (P(None, "radial", "phi", None), P())
    out_specs = (P(None, "radial", "phi", None), P("radial"))
    return jax.shard_map(body, mesh=mesh, in_specs=in_specs, out_specs=out_specs, check_vma=False)
```

time: 99.2 us -> 27.6 us (0.28)
  the two profiles are of different devices: /device:TPU:24 before, /device:TPU:0 now
where the time goes in v1:
time: 27.6 us; the launch traced here: 27.4 us
  Pallas kernels  23.8 us (86%)
  local copies, waits for them, and re-layouts  2.38 us (9%)
  between operations  1.29 us (5%)
    pallas_call x1, Pallas kernels, body(): pl.pallas_call(functools.partial(kernel, sizes, (slabs, wedges)), out_sha...  23.8 us
    unnamed x4, local copies, waits for them, and re-layouts  2.38 us

profile of v1, /device:TPU:0, one launch (start us, length us, event | category | flops | bytes accessed | tf_op | source)
XLA Modules:
  0.0 27.4 jit_solution(11244812318778983407)
XLA Ops:
  1.3 23.8 %shard_map.50 = (f32[8,8,16,128]{3,2,1,0:T(8,128)}, f32[1,8]{1,0:T(1,128)}) custom-call(f32[1]{0:T(128)S(6)} %copy.7.core_ref, f32[8,128]{1,0:T(8,128)} %constant.2.clone.table_ref, f32[8,8,16,128]{3,2,1,0:T(8,128)} %input_ref.1), custom_call_target="tpu_custom_call" | custom-call | tf_op jit(solution)/shard_map/pallas_call | solution.py:413
  25.0 0.0 copy-start
  25.0 1.9 %copy.8 = f32[8,8,16,128]{3,2,1,0:T(8,128)} copy(f32[8,8,16,128]{3,2,1,0:T(8,128)} %get-tuple-element.8) | data formatting | bytes 1048576
  26.9 0.0 copy-done
  26.9 0.5 %copy.9 = f32[8]{0:T(128)} copy(f32[8]{0:T(128)S(1)} %bitcast.1) | data formatting | bytes 64
Async XLA Ops:
  25.0 1.9 %copy-start = (f32[1,8]{1,0:T(1,128)S(1)}, f32[1,8]{1,0:T(1,128)}, u32[]{:S(2)}) copy-start(f32[1,8]{1,0:T(1,128)} %get-tuple-element.5) | copy-start | bytes 100

commit v2 on v1

--- a/solution.py
+++ b/solution.py
@@ -413,8 +413,8 @@
     advanced, mass = pl.pallas_call(
         functools.partial(kernel, sizes, (slabs, wedges)),
         out_shape=(
-            jax.ShapeDtypeStruct(conserved.shape, jnp.float32),
-            jax.ShapeDtypeStruct((1, rows), jnp.float32),
+            pltpu.VMEM(conserved.shape, jnp.float32),
+            pltpu.VMEM((1, rows), jnp.float32),
         ),
         in_specs=[
             pl.BlockSpec(memory_space=pltpu.SMEM), vmem, pl.BlockSpec(memory_space=pl.ANY),

time: 27.6 us -> 25.7 us (0.931)
  local copies, waits for them, and re-layouts: 2.38 us -> 1.31 us
  Pallas kernels: 23.8 us -> 23 us
    unnamed x4 -> x2, local copies, waits for them, and re-layouts: 2.38 us -> 1.31 us
    pallas_call x1, Pallas kernels: 23.8 us -> 23 us  [body(): pl.pallas_call(functools.partial(kernel, sizes, (slabs, wedges)), out_sha...]
where the time goes in v2:
time: 25.7 us; the launch traced here: 25.6 us
  Pallas kernels  23 us (89%)
  local copies, waits for them, and re-layouts  1.31 us (5%)
  between operations  1.28 us (5%)
    pallas_call x1, Pallas kernels, body(): pl.pallas_call(functools.partial(kernel, sizes, (slabs, wedges)), out_sha...  23 us
    unnamed x2, local copies, waits for them, and re-layouts  1.31 us

profile of v2, /device:TPU:0, one launch (start us, length us, event | category | flops | bytes accessed | tf_op | source)
XLA Modules:
  0.0 25.6 jit_solution(10450430552901047477)
XLA Ops:
  1.3 23.0 %shard_map.50 = (f32[8,8,16,128]{3,2,1,0:T(8,128)S(1)}, f32[1,8]{1,0:T(1,128)S(1)}) custom-call(f32[1]{0:T(128)S(6)} %copy.9.core_ref, f32[8,128]{1,0:T(8,128)} %constant.2.clone.table_ref, f32[8,8,16,128]{3,2,1,0:T(8,128)} %input_ref.1), custom_call_target="tpu_custom_call" | custom-call | tf_op jit(solution)/shard_map/pallas_call | solution.py:413
  24.3 0.8 %copy.7 = f32[8,8,16,128]{3,2,1,0:T(8,128)} copy(f32[8,8,16,128]{3,2,1,0:T(8,128)S(1)} %get-tuple-element.6) | data formatting | bytes 1048576
  25.1 0.5 %copy.8 = f32[8]{0:T(128)} copy(f32[8]{0:T(128)S(1)} %bitcast.1) | data formatting | bytes 64

commit v3 on v2

--- a/solution.py
+++ b/solution.py
@@ -99,11 +99,11 @@
     second,
     edge,
     halo,
-    phi_part,
-    phi_got,
-    slab_part,
-    slab_got,
+    part,
+    got,
     pull,
+    table,
+    core,
     load_sem,
     radial_send,
     radial_recv,
@@ -111,8 +111,6 @@
     phi_recv,
     part_send,
     part_recv,
-    slab_send,
-    slab_recv,
 ):
     radial_step, theta_step, phi_step, timestep = sizes
     slabs, wedges = counts
@@ -123,9 +121,13 @@
     has_up, has_down = slab < slabs - 1, slab > 0
 
     load = pltpu.make_async_copy(
-        input_ref, first.at[:, pl.ds(2, rows), pl.ds(PAD, cells), :], load_sem
+        input_ref, first.at[:, pl.ds(2, rows), pl.ds(PAD, cells), :], load_sem.at[0]
     )
     load.start()
+    load_table = pltpu.make_async_copy(table_ref, table, load_sem.at[1])
+    load_table.start()
+    load_core = pltpu.make_async_copy(core_ref, core, load_sem.at[2])
+    load_core.start()
 
     def radial_peer(jump):
         return (lax.rem(slab + jump, slabs), wedge)
@@ -134,11 +136,16 @@
         return (slab, lax.rem(wedge + jump, wedges))
 
     barrier = pltpu.get_barrier_semaphore()
-    peers = [radial_peer(j) for j in range(1, slabs)] + [phi_peer(j) for j in range(1, wedges)]
-    for peer in peers:
-        pl.semaphore_signal(barrier, inc=1, device_id=peer, device_id_type=MESH)
-    pl.semaphore_wait(barrier, len(peers))
+    jumps = [(i, j) for i in range(slabs) for j in range(wedges) if i or j]
+
+    def peer_at(jump):
+        return (radial_peer(jump[0])[0], phi_peer(jump[1])[1])
+
+    for jump in jumps:
+        pl.semaphore_signal(barrier, inc=1, device_id=peer_at(jump), device_id_type=MESH)
     load.wait()
+    load_table.wait()
+    load_core.wait()
 
     def remote(src, dst, send, recv, peer):
         return pltpu.make_async_remote_copy(
@@ -227,39 +234,29 @@
     lane = lax.broadcasted_iota(jnp.int32, (rows, lanes), 1)
     line = lax.broadcasted_iota(jnp.int32, (rows, lanes), 0)
     column = jnp.sum(first[0, pl.ds(2, rows), pl.ds(PAD, cells), :], axis=1)
-    column = jnp.sum(column * table_ref[0:1, :], axis=1, keepdims=True)
+    column = jnp.sum(column * table[0:1, :], axis=1, keepdims=True)
     centres = INNER_RADIUS + (
         (slab * rows + line).astype(jnp.float32) + 0.5
     ) * radial_step
     column = column * centres * centres * (radial_step * theta_step * phi_step)
-    phi_part[...] = jnp.sum(jnp.where(lane == line, column, 0.0), axis=0, keepdims=True)
-    part_copies = [
-        remote(phi_part, phi_got.at[j], part_send.at[j], part_recv.at[j], phi_peer(j))
-        for j in range(1, wedges)
-    ]
-    for copy in part_copies:
-        copy.start()
+    part[...] = jnp.sum(jnp.where(lane == line, column, 0.0), axis=0, keepdims=True)
+    got[0] = part[...]
+    phi_pack(first, 0, 0)
+    phi_pack(first, 0, 1)
+    pl.semaphore_wait(barrier, len(jumps))
+
+    part_copies = []
+    for i, j in jumps:
+        slot = i * wedges + j
+        part_copies.append(
+            remote(part, got.at[slot], part_send.at[slot], part_recv.at[slot], peer_at((i, j)))
+        )
     first_radial = [radial_copies(first, 0, t) for t in range(tiles)]
     second_radial = [radial_copies(second, 1, t) for t in range(tiles)]
-    radial_start(first_radial[0])
-    phi_pack(first, 0, 0)
-    phi_pack(first, 0, 1)
     first_phi, second_phi = phi_copies(0), phi_copies(1)
-    for copy in first_phi:
+    for copy in first_phi + part_copies:
         copy.start()
-
-    total = phi_part[...]
-    for j, copy in enumerate(part_copies, 1):
-        copy.wait_recv()
-        total = total + phi_got[j]
-    slab_part[...] = total
-    slab_copies = [
-        remote(slab_part, slab_got.at[j], slab_send.at[j], slab_recv.at[j], radial_peer(j))
-        for j in range(1, slabs)
-    ]
-    for copy in slab_copies:
-        copy.start()
-    for t in range(1, tiles):
+    for t in range(tiles):
         radial_start(first_radial[t])
 
     lane_tile = lax.broadcasted_iota(jnp.int32, shape, 1)
@@ -284,7 +281,7 @@
         area_in, area_out = inner * inner * scale, outer * outer * scale
         total = [area_in * a - area_out * b for a, b in zip(lower, upper)]
         lower, upper = two_faces([at(r, o) if o else centre for o in range(-2, 3)], 3)
-        around = inverse_r * spread(table_ref[4:5, :])
+        around = inverse_r * spread(table[4:5, :])
         scale = around * (1.0 / phi_step)
         total = [t + (a - b) * scale for t, a, b in zip(total, lower, upper)]
         left, right = [], []
@@ -297,14 +294,14 @@
             right.append(jnp.where(is_last, q, pltpu.roll(q - slope, lanes - 1, 1)))
         upper = flux(left, right, 2)
         scale = around * (1.0 / theta_step)
-        low_sine, high_sine = spread(table_ref[1:2, :]), spread(table_ref[2:3, :])
+        low_sine, high_sine = spread(table[1:2, :]), spread(table[2:3, :])
         low_area, high_area = low_sine * scale, high_sine * scale
         total = [
             t + (low_area * pltpu.roll(f, 1, 1) - high_area * f) for t, f in zip(total, upper)
         ]
         density, inverse, pressure = thermo(centre)
         vr, vt, vp = (centre[m] * inverse for m in (1, 2, 3))
-        cot = spread(table_ref[3:4, :])
+        cot = spread(table[3:4, :])
         total[1] = total[1] + (2.0 * pressure + density * (vt * vt + vp * vp)) * inverse_r
         total[2] = total[2] + (
             (pressure + density * vp * vp) * cot - density * vr * vt
@@ -365,14 +362,22 @@
         phi_unpack(first, 0, side)
     each_row(2, rows - 2, all_tiles(lambda r, t: section_one(r, t, False)))
 
+    for copy in part_copies:
+        copy.wait_recv()
+
+    def slab_shells(jump):
+        shells = jnp.zeros((1, lanes), jnp.float32)
+        for w in range(wedges):
+            shells = shells + got[jump * wedges + lax.rem(wedge + wedges - w, wedges)]
+        return shells
+
     before = jnp.zeros((1, lanes), jnp.float32)
-    for j, copy in enumerate(slab_copies, 1):
-        copy.wait_recv()
-        before = before + jnp.where(slab >= j, slab_got[j], 0.0)
+    for j in range(slabs - 1, 0, -1):
+        before = before + jnp.where(slab >= j, slab_shells(j), 0.0)
     before = jnp.sum(before, axis=1, keepdims=True)
     weight = jnp.where(lane < line, 1.0, jnp.where(lane == line, 0.5, 0.0))
-    within = jnp.sum(weight * slab_part[...], axis=1, keepdims=True)
-    enclosed = core_ref[0] + before + within + jnp.zeros((rows, lanes), jnp.float32)
+    within = jnp.sum(weight * slab_shells(0), axis=1, keepdims=True)
+    enclosed = core[0] + before + within + jnp.zeros((rows, lanes), jnp.float32)
     mass_ref[...] = jnp.sum(jnp.where(lane == line, enclosed, 0.0), axis=0, keepdims=True)[:, :rows]
     pull[...] = strength * enclosed / (centres * centres)
     each_row(2, rows - 2, all_tiles(late_gravity))
@@ -395,7 +400,7 @@
         radial_land(second_radial[t], second, t)
         each_edge(lambda r: section_two(r, t))
 
-    for copy in part_copies + slab_copies + first_phi + second_phi:
+    for copy in part_copies + first_phi + second_phi:
         copy.wait_send()
     for copies in first_radial + second_radial:
         radial_sent(copies)
@@ -416,9 +421,7 @@
             pltpu.VMEM(conserved.shape, jnp.float32),
             pltpu.VMEM((1, rows), jnp.float32),
         ),
-        in_specs=[
-            pl.BlockSpec(memory_space=pltpu.SMEM), vmem, pl.BlockSpec(memory_space=pl.ANY),
-        ],
+        in_specs=[pl.BlockSpec(memory_space=pl.ANY)] * 3,
         out_specs=(vmem, vmem),
         scratch_shapes=[
             pltpu.VMEM(padded, jnp.float32),
@@ -426,19 +429,17 @@
             pltpu.VMEM((4, variables, rows, 2, lanes), jnp.float32),
             pltpu.VMEM((4, variables, rows, 2, lanes), jnp.float32),
             pltpu.VMEM((1, lanes), jnp.float32),
-            pltpu.VMEM((wedges, 1, lanes), jnp.float32),
-            pltpu.VMEM((1, lanes), jnp.float32),
-            pltpu.VMEM((slabs, 1, lanes), jnp.float32),
+            pltpu.VMEM((slabs * wedges, 1, lanes), jnp.float32),
             pltpu.VMEM((rows, lanes), jnp.float32),
-            dma,
+            pltpu.VMEM((TILE, lanes), jnp.float32),
+            pltpu.SMEM((1,), jnp.float32),
+            dma((3,)),
             dma((4 * tiles,)),
             dma((4 * tiles,)),
             dma((4,)),
             dma((4,)),
-            dma((wedges,)),
-            dma((wedges,)),
-            dma((slabs,)),
-            dma((slabs,)),
+            dma((slabs * wedges,)),
+            dma((slabs * wedges,)),
         ],
         compiler_params=pltpu.CompilerParams(collective_id=0, has_side_effects=True),
     )(core_mass, table, conserved)

time: 25.7 us -> 26.3 us (1.023)
  Pallas kernels: 23 us -> 23.6 us
    pallas_call x1, Pallas kernels: 23 us -> 23.6 us  [body(): pl.pallas_call(functools.partial(kernel, sizes, (slabs, wedges)), out_sha...]
where the time goes in v3:
time: 26.3 us; the launch traced here: 26.2 us
  Pallas kernels  23.6 us (90%)
  local copies, waits for them, and re-layouts  1.31 us (5%)
  between operations  1.28 us (5%)
    pallas_call x1, Pallas kernels, body(): pl.pallas_call(functools.partial(kernel, sizes, (slabs, wedges)), out_sha...  23.6 us
    unnamed x2, local copies, waits for them, and re-layouts  1.31 us

profile of v3, /device:TPU:0, one launch (start us, length us, event | category | flops | bytes accessed | tf_op | source)
XLA Modules:
  0.0 26.2 jit_solution(9610136630043211527)
XLA Ops:
  1.3 23.6 %shard_map.50 = (f32[8,8,16,128]{3,2,1,0:T(8,128)S(1)}, f32[1,8]{1,0:T(1,128)S(1)}) custom-call(f32[1]{0:T(128)S(6)} %copy.9.core_ref, f32[8,128]{1,0:T(8,128)} %constant.2.clone.table_ref, f32[8,8,16,128]{3,2,1,0:T(8,128)} %input_ref.1), custom_call_target="tpu_custom_call" | custom-call | tf_op jit(solution)/shard_map/pallas_call | solution.py:418
  24.9 0.8 %copy.7 = f32[8,8,16,128]{3,2,1,0:T(8,128)} copy(f32[8,8,16,128]{3,2,1,0:T(8,128)S(1)} %get-tuple-element.6) | data formatting | bytes 1048576
  25.7 0.5 %copy.8 = f32[8]{0:T(128)} copy(f32[8]{0:T(128)S(1)} %bitcast.1) | data formatting | bytes 64

commit v4 on v3

--- a/solution.py
+++ b/solution.py
@@ -212,23 +212,31 @@
             buffer[:, rows + 2, where, :] = value
             buffer[:, rows + 3, where, :] = value
 
-    def phi_copies(section):
-        slot = section * 2
+    whole, inside, low_edge, high_edge = (0, rows), (2, rows - 4), (0, 2), (rows - 2, 2)
+
+    def phi_copies(section, piece, slot):
+        where = pl.ds(*piece)
         return [
             remote(
-                edge.at[slot + side], halo.at[slot + side], phi_send.at[slot + side],
-                phi_recv.at[slot + side], phi_peer(jump),
+                edge.at[section * 2 + side, :, where], halo.at[section * 2 + side, :, where],
+                phi_send.at[slot + side], phi_recv.at[slot + side], phi_peer(jump),
             )
             for side, jump in ((0, wedges - 1), (1, 1))
         ]
 
-    def phi_pack(buffer, section, side):
+    def phi_pack(buffer, section, side, piece):
+        begin, count = piece
         start = PAD if side == 0 else PAD + cells - 2
-        edge[section * 2 + side] = buffer[:, pl.ds(2, rows), pl.ds(start, 2), :]
-
-    def phi_unpack(buffer, section, side):
+        edge[section * 2 + side, :, pl.ds(begin, count)] = buffer[
+            :, pl.ds(2 + begin, count), pl.ds(start, 2), :
+        ]
+
+    def phi_unpack(buffer, section, side, piece):
+        begin, count = piece
         start = PAD + cells if side == 0 else PAD - 2
-        buffer[:, pl.ds(2, rows), pl.ds(start, 2), :] = halo[section * 2 + side]
+        buffer[:, pl.ds(2 + begin, count), pl.ds(start, 2), :] = halo[
+            section * 2 + side, :, pl.ds(begin, count)
+        ]
 
     shape = (TILE, lanes)
     lane = lax.broadcasted_iota(jnp.int32, (rows, lanes), 1)
@@ -241,8 +249,8 @@
     column = column * centres * centres * (radial_step * theta_step * phi_step)
     part[...] = jnp.sum(jnp.where(lane == line, column, 0.0), axis=0, keepdims=True)
     got[0] = part[...]
-    phi_pack(first, 0, 0)
-    phi_pack(first, 0, 1)
+    phi_pack(first, 0, 0, whole)
+    phi_pack(first, 0, 1, whole)
     pl.semaphore_wait(barrier, len(jumps))
 
     part_copies = []
@@ -253,7 +261,9 @@
         )
     first_radial = [radial_copies(first, 0, t) for t in range(tiles)]
     second_radial = [radial_copies(second, 1, t) for t in range(tiles)]
-    first_phi, second_phi = phi_copies(0), phi_copies(1)
+    first_phi = phi_copies(0, whole, 0)
+    inside_phi = phi_copies(1, inside, 2)
+    low_phi, high_phi = phi_copies(1, low_edge, 4), phi_copies(1, high_edge, 6)
     for copy in first_phi + part_copies:
         copy.start()
     for t in range(tiles):
@@ -262,7 +272,7 @@
     lane_tile = lax.broadcasted_iota(jnp.int32, shape, 1)
     is_first, is_last = lane_tile == 0, lane_tile == lanes - 1
 
-    def rate(buffer, r, tile):
+    def rate(buffer, r, tile, radial=True, rest=True):
         start = PAD + TILE * tile
 
         def at(row, offset):
@@ -276,10 +286,14 @@
         inner, outer = radius - 0.5 * radial_step, radius + 0.5 * radial_step
         inverse_r = 1.0 / radius
         centre = at(r, 0)
-        lower, upper = two_faces([at(r + o, 0) if o else centre for o in range(-2, 3)], 1)
-        scale = inverse_r * inverse_r * (1.0 / radial_step)
-        area_in, area_out = inner * inner * scale, outer * outer * scale
-        total = [area_in * a - area_out * b for a, b in zip(lower, upper)]
+        total = [0.0] * variables
+        if radial:
+            lower, upper = two_faces([at(r + o, 0) if o else centre for o in range(-2, 3)], 1)
+            scale = inverse_r * inverse_r * (1.0 / radial_step)
+            area_in, area_out = inner * inner * scale, outer * outer * scale
+            total = [area_in * a - area_out * b for a, b in zip(lower, upper)]
+        if not rest:
+            return total
         lower, upper = two_faces([at(r, o) if o else centre for o in range(-2, 3)], 3)
         around = inverse_r * spread(table[4:5, :])
         scale = around * (1.0 / phi_step)
@@ -307,20 +321,35 @@
             (pressure + density * vp * vp) * cot - density * vr * vt
         ) * inverse_r
         total[3] = total[3] - density * vp * (vr + vt * cot) * inverse_r
-        return centre, density, total, inverse_r
+        return centre, density, total
 
     def gravity_at(r):
         return jnp.broadcast_to(pull[pl.ds(r, 1), :], shape)
 
-    def section_one(r, tile, with_gravity):
-        centre, density, total, _ = rate(first, r, tile)
-        if with_gravity:
-            gravity = gravity_at(r)
-            total[1] = total[1] - density * gravity
-            total[4] = total[4] - centre[1] * gravity
+    def with_gravity(rates, r):
+        centre, density, total = rates
+        gravity = gravity_at(r)
+        total[1] = total[1] - density * gravity
+        total[4] = total[4] - centre[1] * gravity
+        return centre, total
+
+    def section_one(r, tile):
+        centre, _, total = rate(first, r, tile)
         where = pl.ds(PAD + TILE * tile, TILE)
         for k in range(variables):
             second[k, r + 2, where, :] = centre[k] + timestep * total[k]
+
+    def rest_one(r, tile):
+        centre, total = with_gravity(rate(first, r, tile, radial=False), r)
+        where = pl.ds(PAD + TILE * tile, TILE)
+        for k in range(variables):
+            second[k, r + 2, where, :] = centre[k] + timestep * total[k]
+
+    def radial_one(r, tile):
+        total = rate(first, r, tile, rest=False)
+        where = pl.ds(PAD + TILE * tile, TILE)
+        for k in range(variables):
+            second[k, r + 2, where, :] = second[k, r + 2, where, :] + timestep * total[k]
 
     def late_gravity(r, tile):
         where = pl.ds(PAD + TILE * tile, TILE)
@@ -331,17 +360,20 @@
             second[4, r + 2, where, :] - first[1, r + 2, where, :] * gravity
         )
 
-    def section_two(r, tile):
-        centre, density, total, _ = rate(second, r, tile)
-        gravity = gravity_at(r)
-        total[1] = total[1] - density * gravity
-        total[4] = total[4] - centre[1] * gravity
+    def section_two(r, tile, radial=True):
+        centre, total = with_gravity(rate(second, r, tile, radial=radial), r)
         where = pl.ds(PAD + TILE * tile, TILE)
         into = pl.ds(TILE * tile, TILE)
         for k in range(variables):
             begin = first[k, r + 2, where, :]
             out_ref[k, r, into, :] = 0.5 * begin + 0.5 * (centre[k] + timestep * total[k])
 
+    def radial_two(r, tile):
+        total = rate(second, r, tile, rest=False)
+        into = pl.ds(TILE * tile, TILE)
+        for k in range(variables):
+            out_ref[k, r, into, :] = out_ref[k, r, into, :] + (0.5 * timestep) * total[k]
+
     def each_row(low, high, step):
         lax.fori_loop(low, high, lambda r, _: (step(r), 0)[1], 0)
 
@@ -359,8 +391,8 @@
 
     for side, copy in enumerate(first_phi):
         copy.wait_recv()
-        phi_unpack(first, 0, side)
-    each_row(2, rows - 2, all_tiles(lambda r, t: section_one(r, t, False)))
+        phi_unpack(first, 0, side, whole)
+    each_row(2, rows - 2, all_tiles(section_one))
 
     for copy in part_copies:
         copy.wait_recv()
@@ -381,26 +413,37 @@
     mass_ref[...] = jnp.sum(jnp.where(lane == line, enclosed, 0.0), axis=0, keepdims=True)[:, :rows]
     pull[...] = strength * enclosed / (centres * centres)
     each_row(2, rows - 2, all_tiles(late_gravity))
+    for side, copy in enumerate(inside_phi):
+        phi_pack(second, 1, side, inside)
+        copy.start()
+    each_edge(all_tiles(rest_one))
 
     for t in range(tiles):
         radial_land(first_radial[t], first, t)
-        each_edge(lambda r: section_one(r, t, True))
+        each_edge(lambda r: radial_one(r, t))
         radial_start(second_radial[t])
+        for side, last in ((0, 0), (1, tiles - 1)):
+            if t == last:
+                phi_pack(second, 1, side, low_edge)
+                phi_pack(second, 1, side, high_edge)
+                low_phi[side].start()
+                high_phi[side].start()
         if t == 0:
-            phi_pack(second, 1, 0)
-            second_phi[0].start()
-        if t == tiles - 1:
-            phi_pack(second, 1, 1)
-            second_phi[1].start()
-    for side, copy in enumerate(second_phi):
-        copy.wait_recv()
-        phi_unpack(second, 1, side)
-    each_row(2, rows - 2, all_tiles(section_two))
+            for side, copy in enumerate(inside_phi):
+                copy.wait_recv()
+                phi_unpack(second, 1, side, inside)
+        each_row(2, rows - 2, lambda r: section_two(r, t))
+    for side in range(2):
+        low_phi[side].wait_recv()
+        high_phi[side].wait_recv()
+        phi_unpack(second, 1, side, low_edge)
+        phi_unpack(second, 1, side, high_edge)
+    each_edge(all_tiles(lambda r, t: section_two(r, t, False)))
     for t in range(tiles):
         radial_land(second_radial[t], second, t)
-        each_edge(lambda r: section_two(r, t))
-
-    for copy in part_copies + first_phi + second_phi:
+        each_edge(lambda r: radial_two(r, t))
+
+    for copy in part_copies + first_phi + inside_phi + low_phi + high_phi:
         copy.wait_send()
     for copies in first_radial + second_radial:
         radial_sent(copies)
@@ -436,8 +479,8 @@
             dma((3,)),
             dma((4 * tiles,)),
             dma((4 * tiles,)),
-            dma((4,)),
-            dma((4,)),
+            dma((8,)),
+            dma((8,)),
             dma((slabs * wedges,)),
             dma((slabs * wedges,)),
         ],

time: 26.3 us -> 24.7 us (0.939)
  Pallas kernels: 23.6 us -> 21.9 us
    pallas_call x1, Pallas kernels: 23.6 us -> 21.9 us  [body(): pl.pallas_call(functools.partial(kernel, sizes, (slabs, wedges)), out_sha...]
where the time goes in v4:
time: 24.7 us; the launch traced here: 24.5 us
  Pallas kernels  21.9 us (89%)
  local copies, waits for them, and re-layouts  1.31 us (5%)
  between operations  1.28 us (5%)
    pallas_call x1, Pallas kernels, body(): pl.pallas_call(functools.partial(kernel, sizes, (slabs, wedges)), out_sha...  21.9 us
    unnamed x2, local copies, waits for them, and re-layouts  1.31 us

profile of v4, /device:TPU:0, one launch (start us, length us, event | category | flops | bytes accessed | tf_op | source)
XLA Modules:
  0.0 24.5 jit_solution(13670597162629837846)
XLA Ops:
  1.3 21.9 %shard_map.50 = (f32[8,8,16,128]{3,2,1,0:T(8,128)S(1)}, f32[1,8]{1,0:T(1,128)S(1)}) custom-call(f32[1]{0:T(128)S(6)} %copy.9.core_ref, f32[8,128]{1,0:T(8,128)} %constant.2.clone.table_ref, f32[8,8,16,128]{3,2,1,0:T(8,128)} %input_ref.1), custom_call_target="tpu_custom_call" | custom-call | tf_op jit(solution)/shard_map/pallas_call | solution.py:461
  23.2 0.8 %copy.7 = f32[8,8,16,128]{3,2,1,0:T(8,128)} copy(f32[8,8,16,128]{3,2,1,0:T(8,128)S(1)} %get-tuple-element.6) | data formatting | bytes 1048576
  24.0 0.5 %copy.8 = f32[8]{0:T(128)} copy(f32[8]{0:T(128)S(1)} %bitcast.1) | data formatting | bytes 64

commit v5 on v4

--- a/solution.py
+++ b/solution.py
@@ -100,6 +100,7 @@
     edge,
     halo,
     part,
+    slab_part,
     got,
     pull,
     table,
@@ -136,7 +137,7 @@
         return (slab, lax.rem(wedge + jump, wedges))
 
     barrier = pltpu.get_barrier_semaphore()
-    jumps = [(i, j) for i in range(slabs) for j in range(wedges) if i or j]
+    jumps = [(i, 0) for i in range(1, slabs)] + [(0, j) for j in range(1, wedges)]
 
     def peer_at(jump):
         return (radial_peer(jump[0])[0], phi_peer(jump[1])[1])
@@ -253,9 +254,15 @@
     phi_pack(first, 0, 1, whole)
     pl.semaphore_wait(barrier, len(jumps))
 
+    def wedge_sum():
+        shells = jnp.zeros((1, lanes), jnp.float32)
+        for w in range(wedges):
+            shells = shells + got[lax.rem(wedge + wedges - w, wedges)]
+        return shells
+
     part_copies = []
-    for i, j in jumps:
-        slot = i * wedges + j
+    for j in range(1, wedges):
+        i, slot = 0, j
         part_copies.append(
             remote(part, got.at[slot], part_send.at[slot], part_recv.at[slot], peer_at((i, j)))
         )
@@ -264,9 +271,23 @@
     first_phi = phi_copies(0, whole, 0)
     inside_phi = phi_copies(1, inside, 2)
     low_phi, high_phi = phi_copies(1, low_edge, 4), phi_copies(1, high_edge, 6)
-    for copy in first_phi + part_copies:
+    for copy in part_copies + first_phi:
         copy.start()
-    for t in range(tiles):
+    radial_start(first_radial[0])
+    for copy in part_copies:
+        copy.wait_recv()
+    slab_part[...] = wedge_sum()
+    slab_copies = []
+    for j in range(1, slabs):
+        slot = j * wedges
+        slab_copies.append(
+            remote(
+                slab_part, got.at[slot], part_send.at[slot], part_recv.at[slot], radial_peer(j)
+            )
+        )
+    for copy in slab_copies:
+        copy.start()
+    for t in range(1, tiles):
         radial_start(first_radial[t])
 
     lane_tile = lax.broadcasted_iota(jnp.int32, shape, 1)
@@ -394,21 +415,14 @@
         phi_unpack(first, 0, side, whole)
     each_row(2, rows - 2, all_tiles(section_one))
 
-    for copy in part_copies:
+    for copy in slab_copies:
         copy.wait_recv()
-
-    def slab_shells(jump):
-        shells = jnp.zeros((1, lanes), jnp.float32)
-        for w in range(wedges):
-            shells = shells + got[jump * wedges + lax.rem(wedge + wedges - w, wedges)]
-        return shells
-
     before = jnp.zeros((1, lanes), jnp.float32)
     for j in range(slabs - 1, 0, -1):
-        before = before + jnp.where(slab >= j, slab_shells(j), 0.0)
+        before = before + jnp.where(slab >= j, got[j * wedges], 0.0)
     before = jnp.sum(before, axis=1, keepdims=True)
     weight = jnp.where(lane < line, 1.0, jnp.where(lane == line, 0.5, 0.0))
-    within = jnp.sum(weight * slab_shells(0), axis=1, keepdims=True)
+    within = jnp.sum(weight * slab_part[...], axis=1, keepdims=True)
     enclosed = core[0] + before + within + jnp.zeros((rows, lanes), jnp.float32)
     mass_ref[...] = jnp.sum(jnp.where(lane == line, enclosed, 0.0), axis=0, keepdims=True)[:, :rows]
     pull[...] = strength * enclosed / (centres * centres)
@@ -443,7 +457,7 @@
         radial_land(second_radial[t], second, t)
         each_edge(lambda r: radial_two(r, t))
 
-    for copy in part_copies + first_phi + inside_phi + low_phi + high_phi:
+    for copy in part_copies + slab_copies + first_phi + inside_phi + low_phi + high_phi:
         copy.wait_send()
     for copies in first_radial + second_radial:
         radial_sent(copies)
@@ -472,6 +486,7 @@
             pltpu.VMEM((4, variables, rows, 2, lanes), jnp.float32),
             pltpu.VMEM((4, variables, rows, 2, lanes), jnp.float32),
             pltpu.VMEM((1, lanes), jnp.float32),
+            pltpu.VMEM((1, lanes), jnp.float32),
             pltpu.VMEM((slabs * wedges, 1, lanes), jnp.float32),
             pltpu.VMEM((rows, lanes), jnp.float32),
             pltpu.VMEM((TILE, lanes), jnp.float32),

time: 24.7 us -> 24.3 us (0.984)
  Pallas kernels: 21.9 us -> 21.5 us
    pallas_call x1, Pallas kernels: 21.9 us -> 21.5 us  [body(): pl.pallas_call(functools.partial(kernel, sizes, (slabs, wedges)), out_sha...]
where the time goes in v5:
time: 24.3 us; the launch traced here: 24.1 us
  Pallas kernels  21.5 us (88%)
  local copies, waits for them, and re-layouts  1.31 us (5%)
  between operations  1.28 us (5%)
    pallas_call x1, Pallas kernels, body(): pl.pallas_call(functools.partial(kernel, sizes, (slabs, wedges)), out_sha...  21.5 us
    unnamed x2, local copies, waits for them, and re-layouts  1.31 us

profile of v5, /device:TPU:0, one launch (start us, length us, event | category | flops | bytes accessed | tf_op | source)
XLA Modules:
  0.0 24.1 jit_solution(302091747795731033)
XLA Ops:
  1.3 21.5 %shard_map.50 = (f32[8,8,16,128]{3,2,1,0:T(8,128)S(1)}, f32[1,8]{1,0:T(1,128)S(1)}) custom-call(f32[1]{0:T(128)S(6)} %copy.9.core_ref, f32[8,128]{1,0:T(8,128)} %constant.2.clone.table_ref, f32[8,8,16,128]{3,2,1,0:T(8,128)} %input_ref.1), custom_call_target="tpu_custom_call" | custom-call | tf_op jit(solution)/shard_map/pallas_call | solution.py:475
  22.8 0.8 %copy.7 = f32[8,8,16,128]{3,2,1,0:T(8,128)} copy(f32[8,8,16,128]{3,2,1,0:T(8,128)S(1)} %get-tuple-element.6) | data formatting | bytes 1048576
  23.6 0.5 %copy.8 = f32[8]{0:T(128)} copy(f32[8]{0:T(128)S(1)} %bitcast.1) | data formatting | bytes 64

commit v6 on v5

--- a/solution.py
+++ b/solution.py
@@ -361,7 +361,7 @@
             second[k, r + 2, where, :] = centre[k] + timestep * total[k]
 
     def rest_one(r, tile):
-        centre, total = with_gravity(rate(first, r, tile, radial=False), r)
+        centre, _, total = rate(first, r, tile, radial=False)
         where = pl.ds(PAD + TILE * tile, TILE)
         for k in range(variables):
             second[k, r + 2, where, :] = centre[k] + timestep * total[k]
@@ -414,6 +414,9 @@
         copy.wait_recv()
         phi_unpack(first, 0, side, whole)
     each_row(2, rows - 2, all_tiles(section_one))
+    each_edge(all_tiles(rest_one))
+    radial_land(first_radial[0], first, 0)
+    each_edge(lambda r: radial_one(r, 0))
 
     for copy in slab_copies:
         copy.wait_recv()
@@ -426,15 +429,11 @@
     enclosed = core[0] + before + within + jnp.zeros((rows, lanes), jnp.float32)
     mass_ref[...] = jnp.sum(jnp.where(lane == line, enclosed, 0.0), axis=0, keepdims=True)[:, :rows]
     pull[...] = strength * enclosed / (centres * centres)
-    each_row(2, rows - 2, all_tiles(late_gravity))
-    for side, copy in enumerate(inside_phi):
-        phi_pack(second, 1, side, inside)
-        copy.start()
-    each_edge(all_tiles(rest_one))
-
     for t in range(tiles):
-        radial_land(first_radial[t], first, t)
-        each_edge(lambda r: radial_one(r, t))
+        if t:
+            radial_land(first_radial[t], first, t)
+            each_edge(lambda r: radial_one(r, t))
+        each_edge(lambda r: late_gravity(r, t))
         radial_start(second_radial[t])
         for side, last in ((0, 0), (1, tiles - 1)):
             if t == last:
@@ -443,6 +442,10 @@
                 low_phi[side].start()
                 high_phi[side].start()
         if t == 0:
+            each_row(2, rows - 2, all_tiles(late_gravity))
+            for side, copy in enumerate(inside_phi):
+                phi_pack(second, 1, side, inside)
+                copy.start()
             for side, copy in enumerate(inside_phi):
                 copy.wait_recv()
                 phi_unpack(second, 1, side, inside)

time: 24.3 us -> 26.1 us (1.074)
  Pallas kernels: 21.5 us -> 23.3 us
    pallas_call x1, Pallas kernels: 21.5 us -> 23.3 us  [body(): pl.pallas_call(functools.partial(kernel, sizes, (slabs, wedges)), out_sha...]
where the time goes in v6:
time: 26.1 us; the launch traced here: 25.9 us
  Pallas kernels  23.3 us (89%)
  local copies, waits for them, and re-layouts  1.31 us (5%)
  between operations  1.28 us (5%)
    pallas_call x1, Pallas kernels, body(): pl.pallas_call(functools.partial(kernel, sizes, (slabs, wedges)), out_sha...  23.3 us
    unnamed x2, local copies, waits for them, and re-layouts  1.31 us

profile of v6, /device:TPU:0, one launch (start us, length us, event | category | flops | bytes accessed | tf_op | source)
XLA Modules:
  0.0 25.9 jit_solution(4421135127328584897)
XLA Ops:
  1.3 23.3 %shard_map.50 = (f32[8,8,16,128]{3,2,1,0:T(8,128)S(1)}, f32[1,8]{1,0:T(1,128)S(1)}) custom-call(f32[1]{0:T(128)S(6)} %copy.9.core_ref, f32[8,128]{1,0:T(8,128)} %constant.2.clone.table_ref, f32[8,8,16,128]{3,2,1,0:T(8,128)} %input_ref.1), custom_call_target="tpu_custom_call" | custom-call | tf_op jit(solution)/shard_map/pallas_call | solution.py:478
  24.6 0.8 %copy.7 = f32[8,8,16,128]{3,2,1,0:T(8,128)} copy(f32[8,8,16,128]{3,2,1,0:T(8,128)S(1)} %get-tuple-element.6) | data formatting | bytes 1048576
  25.4 0.5 %copy.8 = f32[8]{0:T(128)} copy(f32[8]{0:T(128)S(1)} %bitcast.1) | data formatting | bytes 64

commit v7 on v6

--- a/solution.py
+++ b/solution.py
@@ -446,10 +446,10 @@
             for side, copy in enumerate(inside_phi):
                 phi_pack(second, 1, side, inside)
                 copy.start()
-            for side, copy in enumerate(inside_phi):
-                copy.wait_recv()
-                phi_unpack(second, 1, side, inside)
-        each_row(2, rows - 2, lambda r: section_two(r, t))
+    for side, copy in enumerate(inside_phi):
+        copy.wait_recv()
+        phi_unpack(second, 1, side, inside)
+    each_row(2, rows - 2, all_tiles(section_two))
     for side in range(2):
         low_phi[side].wait_recv()
         high_phi[side].wait_recv()

time: 26.1 us -> 23.5 us (0.900)
  Pallas kernels: 23.3 us -> 20.8 us
    pallas_call x1, Pallas kernels: 23.3 us -> 20.8 us  [body(): pl.pallas_call(functools.partial(kernel, sizes, (slabs, wedges)), out_sha...]
where the time goes in v7:
time: 23.5 us; the launch traced here: 23.4 us
  Pallas kernels  20.8 us (89%)
  local copies, waits for them, and re-layouts  1.31 us (6%)
  between operations  1.28 us (5%)
    pallas_call x1, Pallas kernels, body(): pl.pallas_call(functools.partial(kernel, sizes, (slabs, wedges)), out_sha...  20.8 us
    unnamed x2, local copies, waits for them, and re-layouts  1.31 us

profile of v7, /device:TPU:0, one launch (start us, length us, event | category | flops | bytes accessed | tf_op | source)
XLA Modules:
  0.0 23.4 jit_solution(6082257044391859857)
XLA Ops:
  1.3 20.8 %shard_map.50 = (f32[8,8,16,128]{3,2,1,0:T(8,128)S(1)}, f32[1,8]{1,0:T(1,128)S(1)}) custom-call(f32[1]{0:T(128)S(6)} %copy.9.core_ref, f32[8,128]{1,0:T(8,128)} %constant.2.clone.table_ref, f32[8,8,16,128]{3,2,1,0:T(8,128)} %input_ref.1), custom_call_target="tpu_custom_call" | custom-call | tf_op jit(solution)/shard_map/pallas_call | solution.py:478
  22.1 0.8 %copy.7 = f32[8,8,16,128]{3,2,1,0:T(8,128)} copy(f32[8,8,16,128]{3,2,1,0:T(8,128)S(1)} %get-tuple-element.6) | data formatting | bytes 1048576
  22.9 0.5 %copy.8 = f32[8]{0:T(128)} copy(f32[8]{0:T(128)S(1)} %bitcast.1) | data formatting | bytes 64
